TPU v7x, 32 devices: a whole 2x2x4 slice. The times are simulated.
32 devices in a mesh: gx: 16 (over z, x, core), gy: 2 (over y).
Axes of the slice: x: 2, y: 2, z: 4, core: 2. Of those that a mesh axis runs over, the one named last changes fastest.
Arguments:
- velocity: float32 [256, 256, 512], P('gx', 'gy'), may hold values from -24 to 24
- viscosity: float32 [256], P('gx'), may hold values from 1000 to 8000
- marker_forces: bfloat16 [4096, 16], P(('gx', 'gy')), may hold values from -18 to 18
- spread_weights: bfloat16 [4096, 16, 2048], P(('gx', 'gy')), may hold values from -1.5 to 1.5
- block_owner: int32 [4096, 1], P(('gx', 'gy')), may hold values from 0 to 31; in each aligned block of 128 rows (0 to 127, 128 to 255, ...) at most 8 rows name the same one
- tile_slot: int32 [4096], P(('gx', 'gy')), may hold values from 0 to 511
Outputs:
- relaxed: float32 [256, 256, 512], P('gx', 'gy')
Inputs may be any that keep to these rules, and one draw needn't show every extreme that they name: `block_owner`: among the 128 blocks held by one device, no owner is named by more than 8 of them.
All inputs are finite; a program needn't handle non-finite values.
Results may differ from a plain program's by a relative error of at most 0.0013.
Values may be sent and summed in bfloat16 or wider, within the bound.
A program may use at most 128 MiB of HBM per device.

v0:
```python
import jax
import jax.numpy as jnp
from jax import lax
from jax.sharding import PartitionSpec as P


def passed_along(x, axis, by):
    length = lax.axis_size(axis)
    pairs = [(i, i + by) for i in range(length) if 0 <= i + by < length]
    return lax.ppermute(x, axis, pairs)


def thomas(below_diag, main_diag, above_diag, right_side):
    count_rows = right_side.shape[0]
    pivot_value = main_diag[0]
    ratios = [above_diag[0] / pivot_value]
    values = [right_side[0] / pivot_value]
    for row_index in range(1, count_rows):
        pivot_value = main_diag[row_index] - below_diag[row_index] * ratios[-1]
        ratios.append(above_diag[row_index] / pivot_value)
        values.append((right_side[row_index] - below_diag[row_index] * values[-1]) / pivot_value)
    result = [values[-1]]
    for row_index in range(count_rows - 2, -1, -1):
        result.append(values[row_index] - ratios[row_index] * result[-1])
    return jnp.stack(result[::-1])


def per_device(velocity, viscosity, marker_forces, spread_weights, block_owner, tile_slot):
    cells_x, cells_y, cells_z = velocity.shape
    line_count = cells_y * cells_z
    grid_x = lax.axis_size("gx")
    grid_y = lax.axis_size("gy")
    devices = grid_x * grid_y
    tile_values = jnp.einsum(
        "bm,bmt->bt", marker_forces, spread_weights, preferred_element_type=jnp.float32
    ).astype(jnp.bfloat16)
    block_count = tile_values.shape[0]
    capacity = max(2, 2 * block_count // devices)
    segment = tile_values.shape[1] // cells_x
    owner_dev = block_owner[:, 0]
    matches = (owner_dev[:, None] == jnp.arange(devices, dtype=jnp.int32)[None, :]).astype(
        jnp.int32
    )
    ranking = jnp.sum(jnp.cumsum(matches, axis=0) * matches, axis=1) - 1
    target = owner_dev * capacity + ranking
    select = target[None, :] == jnp.arange(devices * capacity, dtype=jnp.int32)[:, None]
    outgoing = jnp.dot(
        select.astype(jnp.bfloat16), tile_values, preferred_element_type=jnp.float32
    ).astype(jnp.bfloat16)
    out_slots = (
        jnp.sum(jnp.where(select, tile_slot[None, :], 0), axis=1)
        + jnp.sum(select.astype(jnp.int32), axis=1)
        - 1
    )
    arrived, arrived_slots = (
        lax.all_to_all(
            outgoing.reshape(devices, capacity, -1),
            ("gx", "gy"),
            split_axis=0,
            concat_axis=0,
            tiled=True,
        ),
        lax.all_to_all(
            out_slots.reshape(devices, capacity),
            ("gx", "gy"),
            split_axis=0,
            concat_axis=0,
            tiled=True,
        ),
    )
    positions = line_count // segment
    placing = (
        arrived_slots.reshape(-1)[None, :] == jnp.arange(positions, dtype=jnp.int32)[:, None]
    ).astype(jnp.bfloat16)
    force_field = jnp.einsum(
        "pr,rxs->xps",
        placing,
        arrived.reshape(-1, cells_x, segment),
        preferred_element_type=jnp.float32,
    )
    right_side = velocity.reshape(cells_x, line_count) + force_field.reshape(cells_x, line_count)
    inner_rows = cells_x - 1
    below_diag = -viscosity
    above_diag = -viscosity
    main_diag = 1.0 + 2.0 * viscosity
    interior = thomas(
        below_diag[:inner_rows],
        main_diag[:inner_rows],
        above_diag[:inner_rows],
        right_side[:inner_rows],
    )
    unit_columns = (
        jnp.zeros((inner_rows, 2), jnp.float32).at[0, 0].add(1.0).at[inner_rows - 1, 1].add(1.0)
    )
    spikes = thomas(
        below_diag[:inner_rows], main_diag[:inner_rows], above_diag[:inner_rows], unit_columns
    )
    first_spike = spikes[:, 0]
    last_spike = spikes[:, 1]
    below_first = below_diag[0]
    above_inner = above_diag[inner_rows - 1]
    below_sep = below_diag[inner_rows]
    main_sep = main_diag[inner_rows]
    above_sep = above_diag[inner_rows]
    position = lax.axis_index("gx")
    handed = jnp.stack([below_first * first_spike[0], above_inner * last_spike[0]])
    next_first, next_scalars = passed_along((interior[0], handed), "gx", -1)
    lower_coef = jnp.where(
        position > 0, -below_sep * below_first * first_spike[inner_rows - 1], 0.0
    )
    center_coef = (
        main_sep
        - below_sep * above_inner * last_spike[inner_rows - 1]
        - above_sep * next_scalars[0]
    )
    upper_coef = -above_sep * next_scalars[1]
    reduced_side = (
        right_side[inner_rows] - below_sep * interior[inner_rows - 1] - above_sep * next_first
    )
    coefficients = jnp.stack([lower_coef, center_coef, upper_coef])
    split_coef = lax.all_gather(coefficients, "gx", axis=0, tiled=True).reshape(-1, 3)
    sides = lax.all_to_all(
        reduced_side.reshape(1, grid_x, -1), "gx", split_axis=1, concat_axis=0, tiled=True
    )[:, 0, :]
    separators = lax.linalg.tridiagonal_solve(
        split_coef[:, 0], split_coef[:, 1], split_coef[:, 2], sides
    )
    earlier = jnp.concatenate([jnp.zeros_like(separators[:1]), separators[:-1]], axis=0)
    solved_pairs = jnp.stack([separators, earlier])
    returned = lax.all_to_all(solved_pairs, "gx", split_axis=1, concat_axis=2, tiled=True)
    own_value = returned[0, 0]
    previous = returned[1, 0]
    inner_part = (
        interior
        - below_first * previous[None, :] * first_spike[:, None]
        - above_inner * own_value[None, :] * last_spike[:, None]
    )
    updated = jnp.concatenate([inner_part, own_value[None, :]], axis=0)
    return updated.reshape(velocity.shape)


def solution(mesh):
    placed = (
        P("gx", "gy", None),
        P("gx"),
        P(("gx", "gy"), None),
        P(("gx", "gy"), None, None),
        P(("gx", "gy"), None),
        P(("gx", "gy")),
    )
    return jax.shard_map(
        per_device, mesh=mesh, in_specs=placed, out_specs=P("gx", "gy", None), check_vma=False
    )
```

profile of v0, /device:TPU:0, one launch (start us, length us, event | category | flops | bytes accessed | tf_op | source)
XLA Modules:
  0.0 286.4 jit_solution(17958586952579366199)
XLA Ops:
  3.9 7.3 %all-to-all-start.1 = ((s32[32,1,8]{2,1,0:T(1,128)}), s32[32,1,8]{2,1,0:T(1,128)S(1)}, u32[]{:S(2)}, u32[]{:S(2)}) async-start(s32[32,1,8]{2,1,0:T(1,128)} %bitcast.4), calls=%async_computation.1 | async-start | bytes 32768 | tf_op jit(solution)/shard_map/all_to_all | solution.py:63
  12.1 4.8 %fusion.70 = bf16[128,1,2048]{2,1,0:T(2,128)(2,1)S(1)} fusion(bf16[128,16,1]{1,2,0:T(2,128)(2,1)S(1)} %copy.18, bf16[128,16,2048]{2,1,0:T(8,128)(2,1)} %param.13), kind=kOutput, calls=%fused_computation.197 | convolution fusion | flops 8388608 | bytes 8916992 | tf_op jit(solution)/shard_map/bm,bmt->bt/dot_general | solution.py:34
  18.4 5.8 %all-to-all-start = ((bf16[32,8,2048]{2,1,0:T(8,128)(2,1)}), bf16[32,8,2048]{2,1,0:T(8,128)(2,1)S(1)}, u32[]{:S(2)}, u32[]{:S(2)}) async-start(bf16[32,8,2048]{2,1,0:T(8,128)(2,1)} %fusion), calls=%async_computation | async-start | bytes 2097152 | tf_op jit(solution)/shard_map/all_to_all | solution.py:56
  52.6 8.7 %subtract_divide_fusion.29 = (f32[1,2]{0,1:T(2,128)S(1)}, f32[1,2]{0,1:T(2,128)S(1)}, f32[1,2]{0,1:T(2,128)S(1)}, f32[1,2]{0,1:T(2,128)S(1)}, f32[1,2]{0,1:T(2,1...) fusion(f32[]{:T(128)S(6)} %sub.3676, ...), kind=kLoop, calls=%fused_computation.160 | loop fusion | flops 80 | bytes 220 | tf_op jit(solution)/shard_map/div | solution.py:21
  68.7 6.6 %copy.20 = f32[2,8,128,512]{3,1,2,0:T(8,128)} copy(f32[2,8,128,512]{3,2,1,0:T(8,128)} %bitcast.267) | data formatting | bytes 8388608
  81.8 34.9 %all-reduce.1 = f32[48]{0:T(128)S(1)} all-reduce(f32[48]{0:T(128)S(1)} %maximum_dynamic-update-slice_fusion), channel_id=1, replica_groups=mesh['gx'=16,'gy'=2] {'gx'}, use_global_device_ids=true, to_apply=%add.1 | all-reduce | flops 48 | bytes 384
  149.3 2.7 convolution_bitcast_fusion
  152.1 5.3 %copy.16 = f32[16,512,128]{2,1,0:T(8,128)} copy(f32[16,512,128]{1,2,0:T(8,128)} %convolution_bitcast_fusion) | data formatting | bytes 8388608 | tf_op jit(solution)/shard_map/pr,rxs->xps/transpose | solution.py:75
  157.4 6.0 %bitcast_add_fusion = f32[16,65536]{1,0:T(8,128)S(1)} fusion(f32[16,65536]{1,0:T(8,128)} %bitcast.265, f32[2,8,512,128]{3,2,1,0:T(8,128)} %bitcast.266), kind=kLoop, calls=%fused_computation | loop fusion | flops 1048576 | bytes 12582912 | tf_op jit(solution)/shard_map/add | solution.py:81
  163.4 17.6 %fusion.39 = (f32[65536]{0:T(1024)}, f32[1,65536]{1,0:T(1,128)S(1)}, f32[1,65536]{1,0:T(1,128)S(1)}, f32[1,65536]{1,0:T(1,128)S(1)}, f32[1,65536]{1,0:T(1,128)S(...) fusion(f32[]{:T(128)S(6)} %div.2722, ...), kind=kLoop, calls=%fused_computation.181 | loop fusion | flops 2949120 | bytes 8126584 | tf_op jit(solution)/shard_map/sub | solution.py:24
  181.0 3.3 %fusion.61 = (f32[1,65536]{1,0:T(1,128)S(1)}, f32[1,65536]{1,0:T(1,128)S(1)}, f32[1,65536]{1,0:T(1,128)S(1)}, f32[1,65536]{1,0:T(1,128)S(1)}, f32[1,65536]{1,0:T...) fusion(f32[16,65536]{1,0:T(8,128)S(1)} %bitcast_add_fusion), kind=kLoop, calls=%fused_computation.188 | loop fusion | bytes 7864320 | tf_op jit(solution)/shard_map/slice | solution.py:118
  184.2 10.1 %multiply_subtract_fusion.2 = (f32[65536]{0:T(1024)}, f32[65536]{0:T(1024)}) fusion(f32[65536]{0:T(1024)S(1)} %bitcast.287, f32[]{:T(128)S(6)} %div.2722, f32[]{:T(128)S(6)} %div.2719, f32[]{:T(128)S(6)} %div.2716, f32[]{:T(128)S(6)} %div.2713, f32[]{:T(128)S(6)} %div.2710, f32[]{:T(128)S(6)} %div.2707, f32[]{:T(128)S(6)} %div.2704, f32[]{:T(128)S(6)} %div.2701, ...), kind=kLoop, calls=%fused_computation.16 | loop fusion | flops 4587520 | bytes 4456616 | tf_op jit(solution)/shard_map/sub | solution.py:24
  199.4 1.8 fusion.42
  202.9 1.8 fusion.44
  204.7 2.5 fusion.45
  226.5 6.2 %multiply_subtract_fusion.1 = f32[65536]{0:T(1024)} fusion(f32[65536]{0:T(1024)} %collective-permute-done, f32[65536]{0:T(1024)S(1)} %bitcast.289, f32[]{:T(128)} %bitcast.38, f32[]{:T(128)S(6)} %sub.3678, f32[65536]{0:T(1024)S(1)} %bitcast.271, f32[]{:T(128)S(6)} %sub.3676, f32[65536]{0:T(1024)S(1)} %bitcast.273, f32[]{:T(128)} %bitcast.33, f32[]{:T(128)} %bitcast.35, ...), kind=kLoop, calls=%fused_computation.15 | loop fusion | flops 1441792 | bytes 2621492 | tf_op jit(solution)/shard_map/sub | solution.py:118
  232.6 3.7 %all-to-all-start.2 = ((f32[1,16,4096]{2,0,1:T(1,128)}), f32[1,16,4096]{2,0,1:T(1,128)S(1)}, u32[]{:S(2)}, u32[]{:S(2)}) async-start(f32[1,16,4096]{2,0,1:T(1,128)} %bitcast.54), calls=%async_computation.2 | async-start | bytes 524288 | tf_op jit(solution)/shard_map/all_to_all | solution.py:122
  239.5 6.8 %all-to-all-done.2 = f32[1,16,4096]{2,0,1:T(1,128)S(1)} async-done(((f32[1,16,4096]{2,0,1:T(1,128)}), f32[1,16,4096]{2,0,1:T(1,128)S(1)}, u32[]{:S(2)}, u32[]{:S(2)}) %all-to-all-start.2) | async-done | bytes 262176 | tf_op jit(solution)/shard_map/all_to_all | solution.py:122
  246.3 9.5 %fusion.11 = (f32[1,4096]{1,0:T(1,128)S(1)}, f32[1,4096]{1,0:T(1,128)S(1)}, f32[1,4096]{1,0:T(1,128)S(1)}, f32[1,4096]{1,0:T(1,128)S(1)}, f32[1,4096]{1,0:T(1,12...) fusion(f32[1,16,4096]{2,0,1:T(1,128)S(1)} %all-to-all-done.2, ...), kind=kLoop, calls=%fused_computation.88 | loop fusion | flops 176128 | bytes 491636 | tf_op jit(solution)/shard_map/eval_jaxpr/div | solution.py:125
  259.3 3.8 %all-to-all-start.3 = ((f32[2,16,4096]{2,0,1:T(2,128)}), f32[2,16,4096]{2,0,1:T(2,128)S(1)}, u32[]{:S(2)}, u32[]{:S(2)}) async-start(f32[2,16,4096]{2,0,1:T(2,128)} %pad_maximum_fusion.1), calls=%async_computation.3 | async-start | bytes 1048576 | tf_op jit(solution)/shard_map/all_to_all | solution.py:130
  267.6 9.5 %all-to-all-done.3 = f32[2,16,4096]{2,0,1:T(2,128)S(1)} async-done(((f32[2,16,4096]{2,0,1:T(2,128)}), f32[2,16,4096]{2,0,1:T(2,128)S(1)}, u32[]{:S(2)}, u32[]{:S(2)}) %all-to-all-start.3) | async-done | bytes 524320 | tf_op jit(solution)/shard_map/all_to_all | solution.py:130
  277.1 3.2 %fusion.4 = (f32[16,4096]{1,0:T(8,128)S(1)}, f32[16,4096]{1,0:T(8,128)S(1)}, f32[16,4096]{1,0:T(8,128)S(1)}) fusion(f32[2,16,4096]{2,0,1:T(2,128)S(1)} %all-to-all-done.3, f32[]{:T(128)} %bitcast.8, f32[]{:T(128)} %bitcast.35), kind=kLoop, calls=%fused_computation.12 | loop fusion | flops 131072 | bytes 1310728 | tf_op jit(solution)/shard_map/mul | solution.py:135
  280.5 3.2 %multiply_subtract_fusion = f32[15,128,512]{2,1,0:T(8,128)S(1)} fusion(f32[15,128,512]{2,1,0:T(8,128)} %constant_dynamic-update-slice_fusion, f32[15]{0:T(128)S(1)} %get-tuple-element.186, f32[128,512]{1,0:T(8,128)S(1)} %mul.4323, f32[15]{0:T(128)S(1)} %get-tuple-element.185, f32[128,512]{1,0:T(8,128)S(1)} %mul.4316), kind=kLoop, calls=%fused_computation.2 | loop fusion | flops 3932160 | bytes 8388728 | tf_op jit(solution)/shard_map/sub | solution.py:134
  283.7 2.7 pad_maximum_fusion
  (85 shorter events, 53.4 us)
Async XLA Ops:
  3.9 14.5 %all-to-all-start.1 = ((s32[32,1,8]{2,1,0:T(1,128)}), s32[32,1,8]{2,1,0:T(1,128)S(1)}, u32[]{:S(2)}, u32[]{:S(2)}) async-start(s32[32,1,8]{2,1,0:T(1,128)} %bitcast.4), calls=%async_computation.1 | async-start | bytes 32768 | tf_op jit(solution)/shard_map/all_to_all | solution.py:63
  12.1 12.2 %copy-start.5 = (f32[16]{0:T(128)S(1)}, f32[16]{0:T(128)}, u32[]{:S(2)}) copy-start(f32[16]{0:T(128)} %param.11) | copy-start | bytes 196
  12.1 40.5 %copy-start.3 = (f32[1,2]{0,1:T(2,128)S(1)}, f32[1,2]{0,1:T(2,128)}, u32[]{:S(2)}) copy-start(f32[1,2]{0,1:T(2,128)} %constant.203.clone.1) | copy-start | bytes 28
  16.9 44.4 %copy-start.4 = (f32[1,2]{0,1:T(2,128)S(1)}, f32[1,2]{0,1:T(2,128)}, u32[]{:S(2)}) copy-start(f32[1,2]{0,1:T(2,128)} %constant.201.clone.1) | copy-start | bytes 28
  18.4 130.7 %all-to-all-start = ((bf16[32,8,2048]{2,1,0:T(8,128)(2,1)}), bf16[32,8,2048]{2,1,0:T(8,128)(2,1)S(1)}, u32[]{:S(2)}, u32[]{:S(2)}) async-start(bf16[32,8,2048]{2,1,0:T(8,128)(2,1)} %fusion), calls=%async_computation | async-start | bytes 2097152 | tf_op jit(solution)/shard_map/all_to_all | solution.py:56
  65.7 13.4 %collective-permute-start.1 = (f32[2]{0:T(128)S(1)}, f32[2]{0:T(128)S(1)}, u32[]{:S(2)}, u32[]{:S(2)}) collective-permute-start(f32[2]{0:T(128)S(1)} %pad_maximum_fusion.2), channel_id=1, source_target_pairs={{2,0},{4,2},{6,4},{8,6},{10,8},{12,10},{14,12},{16,14},{18,16},{20... | collective-permute-start | bytes 32 | tf_op jit(solution)/shard_map/ppermute | solution.py:10
  68.7 7.3 %copy-start.6 = (u32[32]{0:T(128)S(1)}, u32[32]{0:T(128)}, u32[]{:S(2)}) copy-start(u32[32]{0:T(128)} %constant.208) | copy-start | bytes 388
  194.4 32.1 %collective-permute-start = (f32[65536]{0:T(1024)}, f32[65536]{0:T(1024)}, u32[]{:S(2)}, u32[]{:S(2)}) collective-permute-start(f32[65536]{0:T(1024)} %get-tuple-element.122), channel_id=1, source_target_pairs={{2,0},{4,2},{6,4},{8,6},{10,8},{12,10},{14,12},{16,14},{18,16},{20... | collective-permute-start | bytes 786440 | tf_op jit(solution)/shard_map/ppermute | solution.py:10
  232.6 30.5 %copy-start.1 = (f32[1,128,512]{2,1,0:T(8,128)S(1)}, f32[1,128,512]{2,1,0:T(8,128)}, u32[]{:S(2)}) copy-start(f32[1,128,512]{2,1,0:T(8,128)} %stack.105) | copy-start | bytes 786436
  232.6 13.6 %all-to-all-start.2 = ((f32[1,16,4096]{2,0,1:T(1,128)}), f32[1,16,4096]{2,0,1:T(1,128)S(1)}, u32[]{:S(2)}, u32[]{:S(2)}) async-start(f32[1,16,4096]{2,0,1:T(1,128)} %bitcast.54), calls=%async_computation.2 | async-start | bytes 524288 | tf_op jit(solution)/shard_map/all_to_all | solution.py:122
  236.3 27.6 %copy-start = (f32[65536]{0:T(1024)S(1)}, f32[65536]{0:T(1024)}, u32[]{:S(2)}) copy-start(f32[65536]{0:T(1024)} %get-tuple-element.52) | copy-start | bytes 786436
  237.0 26.9 %copy-start.2 = (f32[65536]{0:T(1024)S(1)}, f32[65536]{0:T(1024)}, u32[]{:S(2)}) copy-start(f32[65536]{0:T(1024)} %get-tuple-element.36) | copy-start | bytes 786436
  259.3 17.8 %all-to-all-start.3 = ((f32[2,16,4096]{2,0,1:T(2,128)}), f32[2,16,4096]{2,0,1:T(2,128)S(1)}, u32[]{:S(2)}, u32[]{:S(2)}) async-start(f32[2,16,4096]{2,0,1:T(2,128)} %pad_maximum_fusion.1), calls=%async_computation.3 | async-start | bytes 1048576 | tf_op jit(solution)/shard_map/all_to_all | solution.py:130
where the time goes:
time: 289 us; the launch traced here: 286 us
  other arithmetic  86 us (30%)
  between operations  65.1 us (23%)
  local copies, waits for them, and re-layouts  51.5 us (18%)
  blocking collectives  34.9 us (12%)
  starting transfers between devices  23.4 us (8%)
  waiting for transfers between devices  16.3 us (6%)
  matrix products  9.06 us (3%)
    sub x9, other arithmetic, thomas(): result.append(values[row_index] - ratios[row_index] * result[-1])  40.2 us
    unnamed x1, blocking collectives  34.9 us
    unnamed x33, local copies, waits for them, and re-layouts  24.1 us
    another operation x10, local copies, waits for them, and re-layouts, thomas(): return jnp.stack(result[::-1])  11.1 us
    all_to_all x1, waiting for transfers between devices, per_device(): lax.all_to_all(solved_pairs, 'gx', split_axis=1, concat_axis=2, tiled=True)  9.53 us
    div x1, other arithmetic, per_device(): lax.linalg.tridiagonal_solve(split_coef[:, 0], split_coef[:, 1], split_co...  9.47 us
    div x1, other arithmetic, thomas(): (right_side[row_index] - below_diag[row_index] * values[-1]) / pivot_value  8.72 us
    all_to_all x1, starting transfers between devices, per_device(): lax.all_to_all(out_slots.reshape(devices, capacity), ('gx', 'gy'), split_...  7.33 us
  transfers between devices with their start and end apart: 6, of which 2 were waited for; matrix products, arithmetic and copies ran while one was open for 24% of the time, Pallas kernels for 0%

commit v1 on v0

--- a/solution.py
+++ b/solution.py
@@ -119,8 +119,14 @@
     )
     coefficients = jnp.stack([lower_coef, center_coef, upper_coef])
     split_coef = lax.all_gather(coefficients, "gx", axis=0, tiled=True).reshape(-1, 3)
-    sides = lax.all_to_all(
-        reduced_side.reshape(1, grid_x, -1), "gx", split_axis=1, concat_axis=0, tiled=True
+    sides = jnp.concatenate(
+        lax.all_to_all(
+            jnp.stack(jnp.split(reduced_side.reshape(1, grid_x, -1), lax.axis_size("gx"), axis=1)),
+            "gx",
+            0,
+            0,
+        ),
+        axis=0,
     )[:, 0, :]
     separators = lax.linalg.tridiagonal_solve(
         split_coef[:, 0], split_coef[:, 1], split_coef[:, 2], sides

time: 289 us -> 299 us (1.035)
  local copies, waits for them, and re-layouts: 51.5 us -> 62.2 us
    unnamed x33 -> x48, local copies, waits for them, and re-layouts: 24.1 us -> 33.3 us
  transfers between devices with their start and end apart: 6 -> 6, of which waited for: 2 -> 2; matrix products, arithmetic and copies ran while one was open for 24% -> 23% of each run, Pallas kernels for 0% -> 0%
where the time goes in v1:
time: 299 us; the launch traced here: 297 us
  other arithmetic  85.8 us (29%)
  between operations  65 us (22%)
  local copies, waits for them, and re-layouts  62.2 us (21%)
  blocking collectives  34.9 us (12%)
  starting transfers between devices  23.4 us (8%)
  waiting for transfers between devices  16.3 us (5%)
  matrix products  9.06 us (3%)
    sub x9, other arithmetic, thomas(): result.append(values[row_index] - ratios[row_index] * result[-1])  40 us
    unnamed x1, blocking collectives  34.9 us
    unnamed x48, local copies, waits for them, and re-layouts  33.3 us
    another operation x10, local copies, waits for them, and re-layouts, thomas(): return jnp.stack(result[::-1])  11.1 us
    div x1, other arithmetic, per_device(): lax.linalg.tridiagonal_solve(split_coef[:, 0], split_coef[:, 1], split_co...  9.58 us
    all_to_all x1, waiting for transfers between devices, per_device(): lax.all_to_all(solved_pairs, 'gx', split_axis=1, concat_axis=2, tiled=True)  9.53 us
    div x1, other arithmetic, thomas(): (right_side[row_index] - below_diag[row_index] * values[-1]) / pivot_value  8.61 us
    all_to_all x1, starting transfers between devices, per_device(): lax.all_to_all(out_slots.reshape(devices, capacity), ('gx', 'gy'), split_...  7.33 us
  transfers between devices with their start and end apart: 6, of which 2 were waited for; matrix products, arithmetic and copies ran while one was open for 23% of the time, Pallas kernels for 0%

profile of v1, /device:TPU:0, one launch (start us, length us, event | category | flops | bytes accessed | tf_op | source)
XLA Modules:
  0.0 296.8 jit_solution(10901846355051893225)
XLA Ops:
  3.9 7.3 %all-to-all-start.1 = ((s32[32,1,8]{2,1,0:T(1,128)}), s32[32,1,8]{2,1,0:T(1,128)S(1)}, u32[]{:S(2)}, u32[]{:S(2)}) async-start(s32[32,1,8]{2,1,0:T(1,128)} %bitcast.4), calls=%async_computation.1 | async-start | bytes 32768 | tf_op jit(solution)/shard_map/all_to_all | solution.py:63
  12.1 4.8 %fusion.70 = bf16[128,1,2048]{2,1,0:T(2,128)(2,1)S(1)} fusion(bf16[128,16,1]{1,2,0:T(2,128)(2,1)S(1)} %copy.18, bf16[128,16,2048]{2,1,0:T(8,128)(2,1)} %param.13), kind=kOutput, calls=%fused_computation.229 | convolution fusion | flops 8388608 | bytes 8916992 | tf_op jit(solution)/shard_map/bm,bmt->bt/dot_general | solution.py:34
  18.4 5.8 %all-to-all-start = ((bf16[32,8,2048]{2,1,0:T(8,128)(2,1)}), bf16[32,8,2048]{2,1,0:T(8,128)(2,1)S(1)}, u32[]{:S(2)}, u32[]{:S(2)}) async-start(bf16[32,8,2048]{2,1,0:T(8,128)(2,1)} %fusion), calls=%async_computation | async-start | bytes 2097152 | tf_op jit(solution)/shard_map/all_to_all | solution.py:56
  52.3 8.6 %subtract_divide_fusion.29 = (f32[1,2]{0,1:T(2,128)S(1)}, f32[1,2]{0,1:T(2,128)S(1)}, f32[1,2]{0,1:T(2,128)S(1)}, f32[1,2]{0,1:T(2,128)S(1)}, f32[1,2]{0,1:T(2,1...) fusion(f32[]{:T(128)S(6)} %sub.3676, ...), kind=kLoop, calls=%fused_computation.192 | loop fusion | flops 80 | bytes 220 | tf_op jit(solution)/shard_map/div | solution.py:21
  68.2 6.6 %copy.20 = f32[2,8,128,512]{3,1,2,0:T(8,128)} copy(f32[2,8,128,512]{3,2,1,0:T(8,128)} %bitcast.329) | data formatting | bytes 8388608
  81.4 34.9 %all-reduce.1 = f32[48]{0:T(128)S(1)} all-reduce(f32[48]{0:T(128)S(1)} %maximum_dynamic-update-slice_fusion), channel_id=1, replica_groups=mesh['gx'=16,'gy'=2] {'gx'}, use_global_device_ids=true, to_apply=%add.1 | all-reduce | flops 48 | bytes 384
  149.1 2.7 convolution_bitcast_fusion
  151.8 5.3 %copy.16 = f32[16,512,128]{2,1,0:T(8,128)} copy(f32[16,512,128]{1,2,0:T(8,128)} %convolution_bitcast_fusion) | data formatting | bytes 8388608 | tf_op jit(solution)/shard_map/pr,rxs->xps/transpose | solution.py:75
  157.2 6.0 %bitcast_add_fusion = f32[16,65536]{1,0:T(8,128)S(1)} fusion(f32[16,65536]{1,0:T(8,128)} %bitcast.327, f32[2,8,512,128]{3,2,1,0:T(8,128)} %bitcast.328), kind=kLoop, calls=%fused_computation | loop fusion | flops 1048576 | bytes 12582912 | tf_op jit(solution)/shard_map/add | solution.py:81
  163.1 17.5 %fusion.39 = (f32[65536]{0:T(1024)}, f32[1,65536]{1,0:T(1,128)S(1)}, f32[1,65536]{1,0:T(1,128)S(1)}, f32[1,65536]{1,0:T(1,128)S(1)}, f32[1,65536]{1,0:T(1,128)S(...) fusion(f32[]{:T(128)S(6)} %div.2722, ...), kind=kLoop, calls=%fused_computation.213 | loop fusion | flops 2949120 | bytes 8126584 | tf_op jit(solution)/shard_map/sub | solution.py:24
  180.6 3.3 %fusion.61 = (f32[1,65536]{1,0:T(1,128)S(1)}, f32[1,65536]{1,0:T(1,128)S(1)}, f32[1,65536]{1,0:T(1,128)S(1)}, f32[1,65536]{1,0:T(1,128)S(1)}, f32[1,65536]{1,0:T...) fusion(f32[16,65536]{1,0:T(8,128)S(1)} %bitcast_add_fusion), kind=kLoop, calls=%fused_computation.220 | loop fusion | bytes 7864320 | tf_op jit(solution)/shard_map/slice | solution.py:118
  183.9 10.0 %multiply_subtract_fusion.2 = (f32[65536]{0:T(1024)}, f32[65536]{0:T(1024)}) fusion(f32[65536]{0:T(1024)S(1)} %bitcast.349, f32[]{:T(128)S(6)} %div.2722, f32[]{:T(128)S(6)} %div.2719, f32[]{:T(128)S(6)} %div.2716, f32[]{:T(128)S(6)} %div.2713, f32[]{:T(128)S(6)} %div.2710, f32[]{:T(128)S(6)} %div.2707, f32[]{:T(128)S(6)} %div.2704, f32[]{:T(128)S(6)} %div.2701, ...), kind=kLoop, calls=%fused_computation.16 | loop fusion | flops 4587520 | bytes 4456616 | tf_op jit(solution)/shard_map/sub | solution.py:24
  198.9 1.8 fusion.42
  202.4 1.8 fusion.44
  204.1 2.5 fusion.45
  225.9 6.2 %multiply_subtract_fusion.1 = f32[65536]{0:T(1024)} fusion(f32[65536]{0:T(1024)} %collective-permute-done, f32[65536]{0:T(1024)S(1)} %bitcast.351, f32[]{:T(128)} %bitcast.38, f32[]{:T(128)S(6)} %sub.3678, f32[65536]{0:T(1024)S(1)} %bitcast.333, f32[]{:T(128)S(6)} %sub.3676, f32[65536]{0:T(1024)S(1)} %bitcast.335, f32[]{:T(128)} %bitcast.33, f32[]{:T(128)} %bitcast.35, ...), kind=kLoop, calls=%fused_computation.15 | loop fusion | flops 1441792 | bytes 2621492 | tf_op jit(solution)/shard_map/sub | solution.py:118
  242.9 3.7 %all-to-all-start.2 = ((f32[16,1,1,4096]{3,2,1,0:T(1,128)}), f32[16,1,1,4096]{3,2,1,0:T(1,128)S(1)}, u32[]{:S(2)}, u32[]{:S(2)}) async-start(f32[16,1,1,4096]{3,2,1,0:T(1,128)} %constant_dynamic-update-slice_fusion.15), calls=%async_computation.2 | async-start | bytes 524288 | tf_op jit(solution)/shard_map/all_to_all | solution.py:123
  249.7 6.8 %all-to-all-done.2 = f32[16,1,1,4096]{3,2,1,0:T(1,128)S(1)} async-done(((f32[16,1,1,4096]{3,2,1,0:T(1,128)}), f32[16,1,1,4096]{3,2,1,0:T(1,128)S(1)}, u32[]{:S(2)}, u32[]{:S(2)}) %all-to-all-start.2) | async-done | bytes 262176 | tf_op jit(solution)/shard_map/all_to_all | solution.py:123
  256.5 9.6 %fusion.11 = (f32[1,4096]{1,0:T(1,128)S(1)}, f32[1,4096]{1,0:T(1,128)S(1)}, f32[1,4096]{1,0:T(1,128)S(1)}, f32[1,4096]{1,0:T(1,128)S(1)}, f32[1,4096]{1,0:T(1,12...) fusion(f32[16,1,1,4096]{3,2,1,0:T(1,128)S(1)} %all-to-all-done., ...), kind=kLoop, calls=%fused_computation.104 | loop fusion | flops 176128 | bytes 491636 | tf_op jit(solution)/shard_map/eval_jaxpr/div | solution.py:131
  269.6 3.8 %all-to-all-start.3 = ((f32[2,16,4096]{2,0,1:T(2,128)}), f32[2,16,4096]{2,0,1:T(2,128)S(1)}, u32[]{:S(2)}, u32[]{:S(2)}) async-start(f32[2,16,4096]{2,0,1:T(2,128)} %pad_maximum_fusion.1), calls=%async_computation.3 | async-start | bytes 1048576 | tf_op jit(solution)/shard_map/all_to_all | solution.py:136
  277.9 9.5 %all-to-all-done.3 = f32[2,16,4096]{2,0,1:T(2,128)S(1)} async-done(((f32[2,16,4096]{2,0,1:T(2,128)}), f32[2,16,4096]{2,0,1:T(2,128)S(1)}, u32[]{:S(2)}, u32[]{:S(2)}) %all-to-all-start.3) | async-done | bytes 524320 | tf_op jit(solution)/shard_map/all_to_all | solution.py:136
  287.5 3.2 %fusion.4 = (f32[16,4096]{1,0:T(8,128)S(1)}, f32[16,4096]{1,0:T(8,128)S(1)}, f32[16,4096]{1,0:T(8,128)S(1)}) fusion(f32[2,16,4096]{2,0,1:T(2,128)S(1)} %all-to-all-done.3, f32[]{:T(128)} %bitcast.8, f32[]{:T(128)} %bitcast.35), kind=kLoop, calls=%fused_computation.12 | loop fusion | flops 131072 | bytes 1310728 | tf_op jit(solution)/shard_map/mul | solution.py:141
  290.9 3.2 %multiply_subtract_fusion = f32[15,128,512]{2,1,0:T(8,128)S(1)} fusion(f32[15,128,512]{2,1,0:T(8,128)} %constant_dynamic-update-slice_fusion, f32[15]{0:T(128)S(1)} %get-tuple-element.186, f32[128,512]{1,0:T(8,128)S(1)} %mul.4323, f32[15]{0:T(128)S(1)} %get-tuple-element.185, f32[128,512]{1,0:T(8,128)S(1)} %mul.4316), kind=kLoop, calls=%fused_computation.2 | loop fusion | flops 3932160 | bytes 8388728 | tf_op jit(solution)/shard_map/sub | solution.py:140
  294.0 2.7 pad_maximum_fusion
  (102 shorter events, 64.2 us)
Async XLA Ops:
  3.9 14.5 %all-to-all-start.1 = ((s32[32,1,8]{2,1,0:T(1,128)}), s32[32,1,8]{2,1,0:T(1,128)S(1)}, u32[]{:S(2)}, u32[]{:S(2)}) async-start(s32[32,1,8]{2,1,0:T(1,128)} %bitcast.4), calls=%async_computation.1 | async-start | bytes 32768 | tf_op jit(solution)/shard_map/all_to_all | solution.py:63
  12.1 12.2 %copy-start.5 = (f32[16]{0:T(128)S(1)}, f32[16]{0:T(128)}, u32[]{:S(2)}) copy-start(f32[16]{0:T(128)} %param.11) | copy-start | bytes 196
  12.1 40.2 %copy-start.3 = (f32[1,2]{0,1:T(2,128)S(1)}, f32[1,2]{0,1:T(2,128)}, u32[]{:S(2)}) copy-start(f32[1,2]{0,1:T(2,128)} %constant.203.clone.1) | copy-start | bytes 28
  16.9 44.0 %copy-start.4 = (f32[1,2]{0,1:T(2,128)S(1)}, f32[1,2]{0,1:T(2,128)}, u32[]{:S(2)}) copy-start(f32[1,2]{0,1:T(2,128)} %constant.201.clone.1) | copy-start | bytes 28
  18.4 130.4 %all-to-all-start = ((bf16[32,8,2048]{2,1,0:T(8,128)(2,1)}), bf16[32,8,2048]{2,1,0:T(8,128)(2,1)S(1)}, u32[]{:S(2)}, u32[]{:S(2)}) async-start(bf16[32,8,2048]{2,1,0:T(8,128)(2,1)} %fusion), calls=%async_computation | async-start | bytes 2097152 | tf_op jit(solution)/shard_map/all_to_all | solution.py:56
  65.2 13.7 %collective-permute-start.1 = (f32[2]{0:T(128)S(1)}, f32[2]{0:T(128)S(1)}, u32[]{:S(2)}, u32[]{:S(2)}) collective-permute-start(f32[2]{0:T(128)S(1)} %pad_maximum_fusion.2), channel_id=1, source_target_pairs={{2,0},{4,2},{6,4},{8,6},{10,8},{12,10},{14,12},{16,14},{18,16},{20... | collective-permute-start | bytes 32 | tf_op jit(solution)/shard_map/ppermute | solution.py:10
  68.2 7.3 %copy-start.6 = (u32[32]{0:T(128)S(1)}, u32[32]{0:T(128)}, u32[]{:S(2)}) copy-start(u32[32]{0:T(128)} %constant.208) | copy-start | bytes 388
  193.8 32.1 %collective-permute-start = (f32[65536]{0:T(1024)}, f32[65536]{0:T(1024)}, u32[]{:S(2)}, u32[]{:S(2)}) collective-permute-start(f32[65536]{0:T(1024)} %get-tuple-element.122), channel_id=1, source_target_pairs={{2,0},{4,2},{6,4},{8,6},{10,8},{12,10},{14,12},{16,14},{18,16},{20... | collective-permute-start | bytes 786440 | tf_op jit(solution)/shard_map/ppermute | solution.py:10
  242.9 30.6 %copy-start.1 = (f32[1,128,512]{2,1,0:T(8,128)S(1)}, f32[1,128,512]{2,1,0:T(8,128)}, u32[]{:S(2)}) copy-start(f32[1,128,512]{2,1,0:T(8,128)} %stack.156) | copy-start | bytes 786436
  242.9 13.6 %all-to-all-start.2 = ((f32[16,1,1,4096]{3,2,1,0:T(1,128)}), f32[16,1,1,4096]{3,2,1,0:T(1,128)S(1)}, u32[]{:S(2)}, u32[]{:S(2)}) async-start(f32[16,1,1,4096]{3,2,1,0:T(1,128)} %constant_dynamic-update-slice_fusion.15), calls=%async_computation.2 | async-start | bytes 524288 | tf_op jit(solution)/shard_map/all_to_all | solution.py:123
  246.6 27.7 %copy-start = (f32[65536]{0:T(1024)S(1)}, f32[65536]{0:T(1024)}, u32[]{:S(2)}) copy-start(f32[65536]{0:T(1024)} %get-tuple-element.52) | copy-start | bytes 786436
  247.3 27.0 %copy-start.2 = (f32[65536]{0:T(1024)S(1)}, f32[65536]{0:T(1024)}, u32[]{:S(2)}) copy-start(f32[65536]{0:T(1024)} %get-tuple-element.36) | copy-start | bytes 786436
  269.6 17.8 %all-to-all-start.3 = ((f32[2,16,4096]{2,0,1:T(2,128)}), f32[2,16,4096]{2,0,1:T(2,128)S(1)}, u32[]{:S(2)}, u32[]{:S(2)}) async-start(f32[2,16,4096]{2,0,1:T(2,128)} %pad_maximum_fusion.1), calls=%async_computation.3 | async-start | bytes 1048576 | tf_op jit(solution)/shard_map/all_to_all | solution.py:136
